TPU v7x, 8 devices: a whole 2x2x1 slice. The times are simulated.
8 devices in a mesh: data: 8 (over z, y, x, core).
Axes of the slice: x: 2, y: 2, z: 1, core: 2. Of those that a mesh axis runs over, the one named last changes fastest.
Arguments:
- act_in: bfloat16 [8192, 1536], P('data')
- grad_out: bfloat16 [8192, 1536], P('data')
- w_up: bfloat16 [2, 1536, 8960], replicated
- w_down: bfloat16 [2, 8960, 1536], replicated
- master_up: float32 [2, 1536, 8960], P(None, 'data')
- master_down: float32 [2, 8960, 1536], P(None, 'data')
- exp_avg_up: float32 [2, 1536, 8960], P(None, 'data')
- exp_avg_down: float32 [2, 8960, 1536], P(None, 'data')
- exp_sq_up: float32 [2, 1536, 8960], P(None, 'data')
- exp_sq_down: float32 [2, 8960, 1536], P(None, 'data')
- learn_rate: float32 [], replicated
- clip_norm: float32 [], replicated
Outputs:
- output 1: bfloat16 [2, 1536, 8960], replicated
- output 2: bfloat16 [2, 8960, 1536], replicated
- output 3: float32 [2, 1536, 8960], P(None, 'data')
- output 4: float32 [2, 8960, 1536], P(None, 'data')
- output 5: float32 [2, 1536, 8960], P(None, 'data')
- output 6: float32 [2, 8960, 1536], P(None, 'data')
- output 7: float32 [2, 1536, 8960], P(None, 'data')
- output 8: float32 [2, 8960, 1536], P(None, 'data')
- output 9: float32 [], replicated
All inputs are finite; a program needn't handle non-finite values.
Results may differ from a plain program's by a relative error of at most 0.00439.
Values are sent between devices in bfloat16 or wider.
A program may use at most 1.5 GiB of HBM per device.

v0:
```python
import jax
import jax.numpy as jnp
from jax import lax
from jax.sharding import PartitionSpec as P

STEP = 10
BETA_ONE = 0.9
BETA_TWO = 0.95
ADAM_EPS = 1e-8
NORM_EPS = 1e-6
INV_SQRT_TWO = 0.7071067811865476
INV_SQRT_TWO_PI = 0.3989422804014327


def gelu_parts(pre_act):
    normal_cdf = 0.5 * (1.0 + lax.erf(pre_act * INV_SQRT_TWO))
    normal_pdf = jnp.exp(-0.5 * pre_act * pre_act) * INV_SQRT_TWO_PI
    return pre_act * normal_cdf, normal_cdf + pre_act * normal_pdf


def local_grads(act_in, grad_out, w_up, w_down):
    z_one = jnp.einsum("td,df->tf", act_in, w_up[0], preferred_element_type=jnp.float32)
    gelu_one, slope_one = gelu_parts(z_one)
    act_one = gelu_one.astype(jnp.bfloat16)
    hidden = jnp.einsum("tf,fd->td", act_one, w_down[0], preferred_element_type=jnp.float32).astype(jnp.bfloat16)
    z_three = jnp.einsum("td,df->tf", hidden, w_up[1], preferred_element_type=jnp.float32)
    gelu_three, slope_three = gelu_parts(z_three)
    act_three = gelu_three.astype(jnp.bfloat16)
    g_four = jnp.einsum("tf,td->fd", act_three, grad_out, preferred_element_type=jnp.float32)
    dz_three = (jnp.einsum("td,fd->tf", grad_out, w_down[1], preferred_element_type=jnp.float32) * slope_three).astype(jnp.bfloat16)
    g_three = jnp.einsum("td,tf->df", hidden, dz_three, preferred_element_type=jnp.float32)
    d_hidden = jnp.einsum("tf,df->td", dz_three, w_up[1], preferred_element_type=jnp.float32).astype(jnp.bfloat16)
    g_two = jnp.einsum("tf,td->fd", act_one, d_hidden, preferred_element_type=jnp.float32)
    dz_one = (jnp.einsum("td,fd->tf", d_hidden, w_down[0], preferred_element_type=jnp.float32) * slope_one).astype(jnp.bfloat16)
    g_one = jnp.einsum("td,tf->df", act_in, dz_one, preferred_element_type=jnp.float32)
    return g_one, g_two, g_three, g_four


def adam_direction(exp_avg, exp_sq, grad, clip_scale):
    bias_one = 1.0 - BETA_ONE ** STEP
    bias_two = 1.0 - BETA_TWO ** STEP
    avg_new = BETA_ONE * exp_avg + (1.0 - BETA_ONE) * clip_scale * grad
    sq_new = BETA_TWO * exp_sq + (1.0 - BETA_TWO) * (clip_scale * clip_scale) * (grad * grad)
    direction = (avg_new / bias_one) / (jnp.sqrt(sq_new / bias_two) + ADAM_EPS)
    return avg_new, sq_new, direction


def sum_squares(stacked):
    return jnp.sum(stacked * stacked, axis=(1, 2))


def solution(mesh):
    group_size = mesh.shape["data"]
    batch_rows = P("data", None)
    state_rows = P(None, "data", None)
    replicated = P()

    def reduce_rows(grad):
        return lax.psum_scatter(grad, "data", scatter_dimension=0, tiled=True) / group_size

    def device_step(act_in, grad_out, w_up, w_down, master_up, master_down, exp_avg_up, exp_avg_down, exp_sq_up, exp_sq_down, learn_rate, clip_norm):
        g_one, g_two, g_three, g_four = local_grads(act_in, grad_out, w_up, w_down)
        shard_four = reduce_rows(g_four)
        shard_three = reduce_rows(g_three)
        shard_two = reduce_rows(g_two)
        shard_one = reduce_rows(g_one)
        grad_up = jnp.stack([shard_one, shard_three])
        grad_down = jnp.stack([shard_two, shard_four])
        local_sq = jnp.sum(grad_up * grad_up) + jnp.sum(grad_down * grad_down)
        grad_norm = jnp.sqrt(lax.psum(local_sq, "data"))
        clip_scale = jnp.minimum(1.0, clip_norm / (grad_norm + NORM_EPS))
        avg_up, sq_up, dir_up = adam_direction(exp_avg_up, exp_sq_up, grad_up, clip_scale)
        avg_down, sq_down, dir_down = adam_direction(exp_avg_down, exp_sq_down, grad_down, clip_scale)
        local_stats = jnp.concatenate([sum_squares(master_up), sum_squares(master_down), sum_squares(dir_up), sum_squares(dir_down)])
        norm_stats = lax.psum(local_stats, "data")
        trust_ratio = jnp.sqrt(norm_stats[0:4]) / jnp.sqrt(norm_stats[4:8])
        master_up_out = master_up - learn_rate * trust_ratio[0:2, None, None] * dir_up
        master_down_out = master_down - learn_rate * trust_ratio[2:4, None, None] * dir_down
        new_w_up = lax.all_gather(master_up_out.astype(jnp.bfloat16), "data", axis=1, tiled=True)
        new_w_down = lax.all_gather(master_down_out.astype(jnp.bfloat16), "data", axis=1, tiled=True)
        return (new_w_up, new_w_down, master_up_out, master_down_out, avg_up, avg_down, sq_up, sq_down, grad_norm)

    return jax.shard_map(device_step, mesh=mesh, in_specs=(batch_rows, batch_rows, replicated, replicated, state_rows, state_rows, state_rows, state_rows, state_rows, state_rows, replicated, replicated), out_specs=(replicated, replicated, state_rows, state_rows, state_rows, state_rows, state_rows, state_rows, replicated), check_vma=False)
```

profile of v0, /device:TPU:0, one launch (start us, length us, event | category | flops | bytes accessed | tf_op | source)
XLA Modules:
  0.0 2171.4 jit_solution(4744700871585050657)
XLA Ops:
  7.2 1.8 copy-done
  9.1 37.3 %multiply_convert_fusion.1 = (bf16[1024,8960]{1,0:T(8,128)(2,1)}, f32[1024,8960]{1,0:T(8,128)}) fusion(bf16[1024,1536]{1,0:T(8,128)(2,1)S(1)} %copy-done, bf16[2,1536,8960]{2,1,0:T(8,128)(2,1)} %param.14), kind=kOutput, calls=%fused_computation.17 | convolution fusion | flops 28231598080 | bytes 85721088 | tf_op jit(solution)/shard_map/td,df->tf/dot_general | solution.py:22
  46.4 33.5 %fusion.40 = bf16[1024,1536]{1,0:T(8,128)(2,1)S(1)} fusion(bf16[1024,8960]{1,0:T(8,128)(2,1)} %get-tuple-element.39, bf16[2,8960,1536]{2,1,0:T(8,128)(2,1)} %param.15), kind=kOutput, calls=%fused_computation.60 | convolution fusion | flops 28187295744 | bytes 49020928 | tf_op jit(solution)/shard_map/tf,fd->td/dot_general | solution.py:25
  79.9 35.2 %fusion.14 = f32[1024,8960]{1,0:T(8,128)} fusion(bf16[1024,1536]{1,0:T(8,128)(2,1)S(1)} %fusion.40, bf16[2,1536,8960]{2,1,0:T(8,128)(2,1)} %param.14), kind=kOutput, calls=%fused_computation.21 | convolution fusion | flops 28185722880 | bytes 67371008 | tf_op jit(solution)/shard_map/td,df->tf/dot_general | solution.py:26
  115.1 41.8 %fusion.5 = bf16[1024,8960]{1,0:T(8,128)(2,1)} fusion(f32[1024,8960]{1,0:T(8,128)} %fusion.14, bf16[1024,1536]{1,0:T(8,128)(2,1)S(1)} %copy-done.3, bf16[2,8960,1536]{2,1,0:T(8,128)(2,1)} %param.15), kind=kOutput, calls=%fused_computation.8 | convolution fusion | flops 28277473280 | bytes 85721088 | tf_op jit(solution)/shard_map/td,fd->tf/dot_general | solution.py:30
  156.9 36.0 %fusion.50 = f32[1536,8960]{1,0:T(8,128)} fusion(bf16[1024,1536]{1,0:T(8,128)(2,1)S(1)} %fusion.40, bf16[1024,8960]{1,0:T(8,128)(2,1)} %fusion.5), kind=kOutput, calls=%fused_computation.70 | convolution fusion | flops 28185722880 | bytes 76546048
  193.0 36.1 %fusion.43 = bf16[1024,1536]{1,0:T(8,128)(2,1)} fusion(bf16[1024,8960]{1,0:T(8,128)(2,1)} %fusion.5, bf16[2,1536,8960]{2,1,0:T(8,128)(2,1)} %param.14), kind=kOutput, calls=%fused_computation.61 | convolution fusion | flops 28187295744 | bytes 49020928 | tf_op jit(solution)/shard_map/tf,df->td/dot_general | solution.py:32
  229.1 47.6 %fusion.76 = bf16[1024,8960]{1,0:T(8,128)(2,1)S(1)} fusion(f32[1024,8960]{1,0:T(8,128)} %get-tuple-element.40, bf16[1024,1536]{1,0:T(8,128)(2,1)} %fusion.43, bf16[2,8960,1536]{2,1,0:T(8,128)(2,1)} %param.15), kind=kOutput, calls=%fused_computation.14.clone.clone.1 | convolution fusion | flops 28277473280 | bytes 85721088 | tf_op jit(solution)/shard_map/td,fd->tf/dot_general | solution.py:34
  276.7 34.2 %convolution_bitcast_fusion = f32[1536,8960]{0,1:T(8,128)} fusion(bf16[1024,1536]{1,0:T(8,128)(2,1)S(1)} %copy-done, bf16[1024,8960]{1,0:T(8,128)(2,1)S(1)} %fusion.76), kind=kOutput, calls=%fused_computation.2 | convolution fusion | flops 28185722880 | bytes 76546048 | tf_op jit(solution)/shard_map/td,tf->df/dot_general | solution.py:35
  310.9 55.8 %copy.39 = f32[1536,8960]{1,0:T(8,128)} copy(f32[1536,8960]{0,1:T(8,128)} %convolution_bitcast_fusion) | data formatting | bytes 110100480
  366.8 1.8 copy-done.4
  368.6 42.2 %fusion.30 = f32[8960,1536]{1,0:T(8,128)} fusion(bf16[1024,1536]{1,0:T(8,128)(2,1)S(1)} %copy-done.4, f32[1024,8960]{1,0:T(8,128)} %fusion.14), kind=kOutput, calls=%fused_computation.37 | convolution fusion | flops 28231598080 | bytes 94896128 | tf_op jit(solution)/shard_map/tf,td->fd/dot_general | solution.py:29
  410.9 1.9 copy-done.5
  412.8 35.8 %fusion.51 = f32[8960,1536]{1,0:T(8,128)} fusion(bf16[1024,8960]{1,0:T(8,128)(2,1)} %get-tuple-element.39, bf16[1024,1536]{1,0:T(8,128)(2,1)S(1)} %copy-done.5), kind=kOutput, calls=%fused_computation.71 | convolution fusion | flops 28185722880 | bytes 76546048 | tf_op jit(solution)/shard_map/tf,td->fd/dot_general | solution.py:33
  449.4 17.3 copy.29
  466.7 16.9 copy.32
  483.5 6.9 multiply_reduce_fusion.4
  490.5 6.9 multiply_reduce_fusion.3
  497.4 4.0 reduce-scatter.15.cloned.1.call-done
  501.4 8.9 copy.42
  510.3 300.2 %reduce-scatter.13.cloned.1.call-done = f32[192,8960]{1,0:T(8,128)} async-done(((f32[1536,8960]{1,0:T(8,128)}), f32[192,8960]{1,0:T(8,128)}) %reduce-scatter.13.cloned.1.call-update) | async-done | bytes 6881296
  810.5 8.9 copy.40
  819.4 300.8 %reduce-scatter.11.cloned.1.call-done = f32[1120,1536]{1,0:T(8,128)} async-done(((f32[8960,1536]{1,0:T(8,128)}), f32[1120,1536]{1,0:T(8,128)}) %reduce-scatter.11.cloned.1.call-update) | async-done | bytes 6881296 | tf_op jit(solution)/shard_map/reduce_scatter | solution.py:59
  1120.2 7.5 multiply_bitcast_fusion.2
  1127.7 5.4 multiply_bitcast_fusion
  1133.1 1.9 slice-done.4
  1135.1 0.5 slice-done.5
  1135.6 5.9 multiply_bitcast_fusion.1
  1141.5 287.7 %reduce-scatter.9.cloned.1.call-done = f32[1120,1536]{1,0:T(8,128)} async-done(((f32[8960,1536]{1,0:T(8,128)}), f32[1120,1536]{1,0:T(8,128)}) %reduce-scatter.9.cloned.1.call-update) | async-done | bytes 6881296 | tf_op jit(solution)/shard_map/reduce_scatter | solution.py:59
  1429.2 6.8 multiply_bitcast_fusion.3
  1436.0 9.2 multiply_reduce_fusion.5
  1445.1 7.6 multiply_reduce_fusion.1
  1454.0 16.6 copy.31
  1470.7 22.6 %psum.14 = f32[]{:T(128)} all-reduce(f32[]{:T(128)S(6)} %add.58), channel_id=1, replica_groups=mesh['data'=8] {'data'}, use_global_device_ids=true, to_apply=%region_8.0 | all-reduce | flops 1 | bytes 8 | tf_op jit(solution)/shard_map/psum | solution.py:70
  1494.0 37.8 %multiply_reduce_fusion = (f32[2]{0:T(128)S(1)}, f32[2,192,8960]{1,2,0:T(8,128)}, f32[2,192,8960]{1,2,0:T(8,128)}) fusion(f32[1,192,8960]{1,2,0:T(8,128)} %multiply_bitcast_fusion, f32[1,192,8960]{1,2,0:T(8,128)} %multiply_bitcast_fusion.1, f32[]{:T(128)S(6)} %mul.179, f32[2,192,8960]{1,2,0:T(8,128)} %copy.29, f32[]{:T(128)S(6)} %mul.185, ...), kind=kLoop, calls=%fused_computation.40 | loop fusion | flops 48168960 | bytes 68812816 | tf_op jit(solution)/shard_map/reduce_sum | solution.py:49
  1531.8 27.2 %multiply_reduce_fusion.2 = (f32[2]{0:T(128)S(1)}, f32[2,1120,1536]{2,1,0:T(8,128)}, f32[2,1120,1536]{2,1,0:T(8,128)}) fusion(f32[1,1120,1536]{2,1,0:T(8,128)} %multiply_bitcast_fusion.2, f32[1,1120,1536]{2,1,0:T(8,128)} %multiply_bitcast_fusion.3, f32[]{:T(128)S(6)} %mul.179, f32[2,1120,1536]{2,1,0:T(8,128)} %param.19, f32[]{:T(128)S(6)} %mul.185, ...), kind=kLoop, calls=%fused_computation.49 | loop fusion | flops 48168960 | bytes 68812816 | tf_op jit(solution)/shard_map/reduce_sum | solution.py:49
  1559.8 24.2 %psum.15 = f32[8]{0:T(128)S(1)} all-reduce(f32[8]{0:T(128)S(1)} %pad_maximum_fusion.2), channel_id=1, replica_groups=mesh['data'=8] {'data'}, use_global_device_ids=true, to_apply=%region_11.0 | all-reduce | flops 8 | bytes 64 | tf_op jit(solution)/shard_map/psum | solution.py:75
  1584.1 28.9 %fusion.49 = (bf16[2,192,8960]{1,2,0:T(8,128)(2,1)}, f32[2,192,8960]{1,2,0:T(8,128)}) fusion(f32[2,192,8960]{1,2,0:T(8,128)} %copy.32, f32[2,192,8960]{1,2,0:T(8,128)} %get-tuple-element.33, f32[2,192,8960]{1,2,0:T(8,128)} %get-tuple-element.32, f32[2]{0:T(128)S(1)} %get-tuple-element.38), kind=kLoop, calls=%fused_computation.69 | loop fusion | flops 24084480 | bytes 61931528 | tf_op jit(solution)/shard_map/convert_element_type | solution.py:79
  1613.0 17.2 copy.33
  1630.3 27.4 %fusion.48 = (bf16[2,1120,1536]{2,1,0:T(8,128)(2,1)}, f32[2,1120,1536]{2,1,0:T(8,128)}) fusion(f32[2,1120,1536]{2,1,0:T(8,128)} %param.17, f32[2,1120,1536]{2,1,0:T(8,128)} %get-tuple-element.57, f32[2,1120,1536]{2,1,0:T(8,128)} %get-tuple-element.55, f32[2]{0:T(128)S(1)} %get-tuple-element.37), kind=kLoop, calls=%fused_computation.68 | loop fusion | flops 24084480 | bytes 61931528 | tf_op jit(solution)/shard_map/convert_element_type | solution.py:80
  1657.7 16.9 copy.36
  1674.6 16.9 copy.37
  1691.4 16.9 copy.35
  1708.3 169.1 %all-gather.3.cloned.1.call-done = bf16[2,1536,8960]{2,0,1:T(2,128)(2,1)} async-done(((bf16[2,192,8960]{2,0,1:T(2,128)(2,1)}), bf16[2,1536,8960]{2,0,1:T(2,128)(2,1)}) %all-gather.3.cloned.1.call-update) | async-done | bytes 55050256 | tf_op jit(solution)/shard_map/all_gather | solution.py:79
  1877.4 40.4 %copy.34 = bf16[2,1536,8960]{2,1,0:T(8,128)(2,1)} copy(bf16[2,1536,8960]{2,0,1:T(2,128)(2,1)} %all-gather.3.cloned.1.call-done) | data formatting | bytes 110100480
  1917.8 207.5 %all-gather.5.cloned.1.call-done = bf16[2,8960,1536]{2,1,0:T(8,128)(2,1)} async-done(((bf16[2,1120,1536]{2,1,0:T(8,128)(2,1)}), bf16[2,8960,1536]{2,1,0:T(8,128)(2,1)}) %all-gather.5.cloned.1.call-update) | async-done | bytes 55050256 | tf_op jit(solution)/shard_map/all_gather | solution.py:80
  2125.3 37.0 %copy.46 = bf16[2,8960,1536]{2,1,0:T(8,128)(2,1)} copy(bf16[2,8960,1536]{2,1,0:T(8,128)(2,1)} %all-gather.5.cloned.1.call-done) | data formatting | bytes 110100480
  2162.3 1.0 copy-done.1
  (35 shorter events, 0.6 us)
Async XLA Ops:
  7.2 1.9 copy-start
  7.2 494.2 %reduce-scatter.15.cloned.1.call-start = ((), (), s32[]{:S(2)}) async-start(), calls=%async_computation.9 | async-start | bytes 61931520
  79.9 35.2 %copy-start.3 = (bf16[1024,1536]{1,0:T(8,128)(2,1)S(1)}, bf16[1024,1536]{1,0:T(8,128)(2,1)}, u32[]{:S(2)}) copy-start(bf16[1024,1536]{1,0:T(8,128)(2,1)} %param.13) | copy-start | bytes 9437188
  192.9 617.6 %reduce-scatter.13.cloned.1.call-start = ((), (), s32[]{:S(2)}) async-start(), calls=%async_computation.8 | async-start | bytes 61931520
  366.7 1.9 copy-start.4
  366.7 753.5 %reduce-scatter.11.cloned.1.call-start = ((), (), s32[]{:S(2)}) async-start(), calls=%async_computation.5 | async-start | bytes 61931520 | tf_op jit(solution)/shard_map/reduce_scatter | solution.py:59
  410.8 2.0 copy-start.5
  410.8 1018.3 %reduce-scatter.9.cloned.1.call-start = ((), (), s32[]{:S(2)}) async-start(), calls=%async_computation.4 | async-start | bytes 61931520 | tf_op jit(solution)/shard_map/reduce_scatter | solution.py:59
  448.7 1428.8 %all-gather.3.cloned.1.call-start = ((), (), s32[]{:S(2)}) async-start(), calls=%async_computation.6 | async-start | bytes 61931520 | tf_op jit(solution)/shard_map/all_gather | solution.py:79
  1120.2 7.5 copy-start.2
  1120.2 12.9 slice-start.3
  1120.2 14.9 slice-start.4
  1127.7 7.9 slice-start.5
  1429.2 16.0 slice-start
  1429.2 16.0 slice-start.1
  1436.0 9.2 slice-start.2
  1630.2 495.1 %all-gather.5.cloned.1.call-start = ((), (), s32[]{:S(2)}) async-start(), calls=%async_computation.7 | async-start | bytes 61931520 | tf_op jit(solution)/shard_map/all_gather | solution.py:80
  2125.3 38.0 %copy-start.1 = (bf16[1024,1536]{1,0:T(8,128)(2,1)S(1)}, bf16[1024,1536]{1,0:T(8,128)(2,1)}, u32[]{:S(2)}) copy-start(bf16[1024,1536]{1,0:T(8,128)(2,1)} %param.12) | copy-start | bytes 9437188
Sparse Core Ops, SparseCore 0:
  193.0 308.3 reduce-scatter.14
  504.9 305.5 reduce-scatter.12
  814.6 305.5 reduce-scatter.10
  1123.6 305.5 reduce-scatter.8
  1630.3 247.0 all-gather.2
  1879.1 246.1 all-gather.4
where the time goes:
time: 2180 us; the launch traced here: 2170 us
  waiting for transfers between devices  1270 us (58%)
  matrix products  380 us (17%)
  local copies, waits for them, and re-layouts  279 us (13%)
  other arithmetic  178 us (8%)
  blocking collectives  46.8 us (2%)
    reduce_scatter x2, waiting for transfers between devices, reduce_rows(): lax.psum_scatter(grad, 'data', scatter_dimension=0, tiled=True) / group_size  589 us
    unnamed x8, waiting for transfers between devices  304 us
    unnamed x35, local copies, waits for them, and re-layouts  261 us
    all_gather x1, waiting for transfers between devices, device_step(): lax.all_gather(master_down_out.astype(jnp.bfloat16), 'data', axis=1, tile...  208 us
    all_gather x1, waiting for transfers between devices, device_step(): lax.all_gather(master_up_out.astype(jnp.bfloat16), 'data', axis=1, tiled=...  169 us
    reduce_sum x4, other arithmetic, sum_squares(): return jnp.sum(stacked * stacked, axis=(1, 2))  78.9 us
    dot_general x1, matrix products, local_grads(): jnp.einsum('td,fd->tf', d_hidden, w_down[0], preferred_element_type=jnp.f...  47.6 us
  transfers between devices with their start and end apart: 6, of which 6 were waited for; matrix products, arithmetic and copies ran while one was open for 21% of the time, Pallas kernels for 0%

commit v1 on v0

v1 whole, which is shorter than its diff:
```python
import functools

import jax
import jax.numpy as jnp
from jax import lax
from jax.experimental import pallas as pl
from jax.experimental.pallas import tpu as pltpu
from jax.sharding import PartitionSpec as P


STEP = 10
BETA_ONE = 0.9
BETA_TWO = 0.95
ADAM_EPS = 1e-8
NORM_EPS = 1e-6
INV_SQRT_TWO = 0.7071067811865476
INV_SQRT_TWO_PI = 0.3989422804014327
INV_BIAS_ONE = 1.0 / (1.0 - BETA_ONE ** STEP)
INV_BIAS_TWO = 1.0 / (1.0 - BETA_TWO ** STEP)

MESH = pl.DeviceIdType.MESH
ANY = pl.BlockSpec(memory_space=pl.ANY)
SMEM = pl.BlockSpec(memory_space=pltpu.SMEM)
BF = jnp.bfloat16


def gelu_val(pre_act):
    return pre_act * (0.5 * (1.0 + lax.erf(pre_act * INV_SQRT_TWO)))


def gelu_slope(pre_act):
    normal_cdf = 0.5 * (1.0 + lax.erf(pre_act * INV_SQRT_TWO))
    normal_pdf = jnp.exp(-0.5 * pre_act * pre_act) * INV_SQRT_TWO_PI
    return normal_cdf + pre_act * normal_pdf


def mm(spec, lhs, rhs):
    return jnp.einsum(spec, lhs, rhs, preferred_element_type=jnp.float32)


def params(mib=48, **kw):
    return pltpu.CompilerParams(vmem_limit_bytes=mib << 20, **kw)


def psum_kernel(n, x_ref, o_ref, buf, send_sem, recv_sem):
    me = lax.axis_index("data")
    barrier = pltpu.get_barrier_semaphore()
    for d in range(1, n):
        pl.semaphore_signal(barrier, inc=1, device_id=(lax.bitwise_xor(me, d),), device_id_type=MESH)
    pl.semaphore_wait(barrier, n - 1)
    copies = []
    for d in range(1, n):
        copy = pltpu.make_async_remote_copy(
            src_ref=x_ref, dst_ref=buf.at[me], send_sem=send_sem.at[d], recv_sem=recv_sem.at[d],
            device_id=(lax.bitwise_xor(me, d),), device_id_type=MESH)
        copy.start()
        copies.append(copy)
    buf[me] = x_ref[...]
    for copy in copies:
        copy.wait()
    total = buf[0]
    for d in range(1, n):
        total = total + buf[d]
    for k in range(x_ref.shape[0]):
        o_ref[k] = jnp.sum(total[k])


def device_sums(parts, n, collective_id):
    k = parts.shape[0]
    return pl.pallas_call(
        functools.partial(psum_kernel, n),
        out_shape=jax.ShapeDtypeStruct((k,), jnp.float32),
        in_specs=[pl.BlockSpec(memory_space=pltpu.VMEM)],
        out_specs=SMEM,
        scratch_shapes=[pltpu.VMEM((n, k, 8, 128), jnp.float32), pltpu.SemaphoreType.DMA((n,)), pltpu.SemaphoreType.DMA((n,))],
        compiler_params=pltpu.CompilerParams(collective_id=collective_id, has_side_effects=True),
    )(parts)


def direction(avg_new, sq_new):
    return (avg_new * INV_BIAS_ONE) / (jnp.sqrt(sq_new * INV_BIAS_TWO) + ADAM_EPS)


def fold(x):
    rows, cols = x.shape
    return jnp.sum(jnp.sum(x.reshape(rows // 8, 8, cols), axis=0).reshape(8, cols // 128, 128), axis=1)


def moments(s_ref, g, m_ref, v_ref, mo_ref, vo_ref, acc_ref, first):
    s = s_ref[0]
    m = BETA_ONE * m_ref[0] + ((1.0 - BETA_ONE) * s) * g
    v = BETA_TWO * v_ref[0] + ((1.0 - BETA_TWO) * (s * s)) * (g * g)
    mo_ref[0] = m
    vo_ref[0] = v
    u = direction(m, v)

    @pl.when(first)
    def _():
        acc_ref[...] = jnp.zeros_like(acc_ref)

    acc_ref[0] += fold(u * u)


def moments_down_kernel(s_ref, ga_ref, gb_ref, m_ref, v_ref, mo_ref, vo_ref, acc_ref):
    k = pl.program_id(0)
    g = jnp.where(k == 0, ga_ref[...], gb_ref[...])
    moments(s_ref, g, m_ref, v_ref, mo_ref, vo_ref, acc_ref, pl.program_id(1) == 0)


def moments_down(scale, g_a, g_b, m, v, rows):
    _, total, cols = m.shape
    blocks = total // rows
    state = pl.BlockSpec((1, rows, cols), lambda k, i: (k, i, 0))
    return pl.pallas_call(
        moments_down_kernel,
        grid=(2, blocks),
        out_shape=(jax.ShapeDtypeStruct(m.shape, m.dtype), jax.ShapeDtypeStruct(v.shape, v.dtype), jax.ShapeDtypeStruct((2, 8, 128), jnp.float32)),
        in_specs=[SMEM,
                  pl.BlockSpec((rows, cols), lambda k, i: (jnp.where(k == 0, i, blocks - 1), 0)),
                  pl.BlockSpec((rows, cols), lambda k, i: (jnp.where(k == 0, 0, i), 0)),
                  state, state],
        out_specs=(state, state, pl.BlockSpec((1, 8, 128), lambda k, i: (k, 0, 0))),
        compiler_params=params(),
        cost_estimate=pl.CostEstimate(flops=40 * m.size, bytes_accessed=20 * m.size, transcendentals=2 * m.size),
        name="moments_down",
    )(scale, g_a, g_b, m, v)


def moments_up_kernel(s_ref, g_ref, m_ref, v_ref, *rest):
    mo_ref, vo_ref, acc_ref, g_scr = rest[-4:]
    parts, _, width = g_ref.shape
    for p in range(parts):
        g_scr[:, p * width:(p + 1) * width] = g_ref[p]
    moments(s_ref, g_scr[...], m_ref, v_ref, mo_ref, vo_ref, acc_ref, pl.program_id(0) == 0)


def moments_up(scale, g_parts, m, v, which, into, rows):
    _, total, cols = m.shape
    n, _, width = g_parts.shape
    state = pl.BlockSpec((1, rows, cols), lambda i: (which, i, 0))
    extra = [] if into is None else list(into)
    return pl.pallas_call(
        moments_up_kernel,
        grid=(total // rows,),
        out_shape=(jax.ShapeDtypeStruct(m.shape, m.dtype), jax.ShapeDtypeStruct(v.shape, v.dtype), jax.ShapeDtypeStruct((1, 8, 128), jnp.float32)),
        in_specs=[SMEM, pl.BlockSpec((n, rows, width), lambda i: (0, i, 0)), state, state] + [ANY] * len(extra),
        out_specs=(state, state, pl.BlockSpec((1, 8, 128), lambda i: (0, 0, 0))),
        scratch_shapes=[pltpu.VMEM((rows, cols), jnp.float32)],
        input_output_aliases={} if into is None else {4: 0, 5: 1},
        compiler_params=params(),
        cost_estimate=pl.CostEstimate(flops=20 * m.size, bytes_accessed=10 * m.size, transcendentals=m.size),
    )(scale, g_parts, m, v, *extra)


def apply_kernel(f_ref, p_ref, m_ref, v_ref, *rest):
    po_ref, w_ref = rest[-2:]
    new = p_ref[0] - f_ref[0] * direction(m_ref[0], v_ref[0])
    po_ref[0] = new
    w_ref[...] = new.astype(w_ref.dtype)


def apply_update(factor, master, m, v, which, into, rows):
    _, total, cols = m.shape
    state = pl.BlockSpec((1, rows, cols), lambda i: (which, i, 0))
    extra = [] if into is None else [into]
    return pl.pallas_call(
        apply_kernel,
        grid=(total // rows,),
        out_shape=(jax.ShapeDtypeStruct(m.shape, m.dtype), jax.ShapeDtypeStruct((total, cols), BF)),
        in_specs=[SMEM, state, state, state] + [ANY] * len(extra),
        out_specs=(state, pl.BlockSpec((rows, cols), lambda i: (i, 0))),
        input_output_aliases={} if into is None else {4: 0},
        compiler_params=params(),
        cost_estimate=pl.CostEstimate(flops=15 * m.size, bytes_accessed=9 * m.size, transcendentals=m.size),
    )(factor, master, m, v, *extra)


def ag_kernel(count, *refs):
    ins, outs = refs[:count], refs[count:2 * count]
    send_sem, recv_sem, local_sem = refs[2 * count:]
    me = lax.axis_index("data")
    core, nx, ny, nd = (lax.bitwise_xor(me, b) for b in (1, 2, 4, 6))
    barrier = pltpu.get_barrier_semaphore()
    for peer in (core, nx, ny):
        pl.semaphore_signal(barrier, inc=1, device_id=(peer,), device_id_type=MESH)
    pl.semaphore_wait(barrier, 3)

    def rows(a, owner, half):
        height = ins[a].shape[0]
        first = (height // 2 + 15) // 16 * 16
        if half is None:
            return pl.ds(owner * height, height)
        start, size = (0, first) if half == 0 else (first, height - first)
        return pl.ds(owner * height + start, size)

    def own(a, half):
        height = ins[a].shape[0]
        first = (height // 2 + 15) // 16 * 16
        if half is None:
            return ins[a]
        return ins[a].at[pl.ds(0, first)] if half == 0 else ins[a].at[pl.ds(first, height - first)]

    def copy(a, slot, src, owner, half, peer):
        return pltpu.make_async_remote_copy(
            src_ref=src, dst_ref=outs[a].at[rows(a, owner, half)], send_sem=send_sem.at[a, slot], recv_sem=recv_sem.at[a, slot],
            device_id=(peer,), device_id_type=MESH)

    def held(a, owner, half):
        return outs[a].at[rows(a, owner, half)]

    arrays = range(count)
    local = [pltpu.make_async_copy(ins[a], held(a, me, None), local_sem.at[a]) for a in arrays]
    started = []

    def go(c):
        c.start()
        started.append(c)
        return c

    x_first = [go(copy(a, 0, own(a, 0), me, 0, nx)) for a in arrays]
    y_first = [go(copy(a, 1, own(a, 1), me, 1, ny)) for a in arrays]
    x_second = [go(copy(a, 2, own(a, 1), me, 1, nx)) for a in arrays]
    y_second = [go(copy(a, 3, own(a, 0), me, 0, ny)) for a in arrays]
    c_own = [go(copy(a, 4, ins[a], me, None, core)) for a in arrays]
    for c in local:
        c.start()
    y_third, x_third = [], []
    for a in arrays:
        x_first[a].wait_recv()
        y_third.append(go(copy(a, 5, held(a, nx, 0), nx, 0, ny)))
        go(copy(a, 7, held(a, nx, 0), nx, 0, core))
        y_first[a].wait_recv()
        x_third.append(go(copy(a, 6, held(a, ny, 1), ny, 1, nx)))
        go(copy(a, 8, held(a, ny, 1), ny, 1, core))
    for a in arrays:
        x_second[a].wait_recv()
        go(copy(a, 9, held(a, nx, 1), nx, 1, core))
        y_second[a].wait_recv()
        go(copy(a, 10, held(a, ny, 0), ny, 0, core))
    for a in arrays:
        y_third[a].wait_recv()
        go(copy(a, 11, held(a, nd, 0), nd, 0, core))
        x_third[a].wait_recv()
        go(copy(a, 12, held(a, nd, 1), nd, 1, core))
    for c in c_own:
        c.wait_recv()
    for c in started:
        c.wait_send()
    for a in arrays:
        for slot in range(7, 13):
            half = 0 if slot in (7, 10, 11) else 1
            copy(a, slot, held(a, me, half), me, half, core).wait_recv()
    for c in local:
        c.wait()


def gather_rows(shards, n, collective_id):
    count = len(shards)
    return pl.pallas_call(
        functools.partial(ag_kernel, count),
        out_shape=[jax.ShapeDtypeStruct((n * s.shape[0],) + s.shape[1:], s.dtype) for s in shards],
        in_specs=[ANY] * count,
        out_specs=[ANY] * count,
        scratch_shapes=[pltpu.SemaphoreType.DMA((count, 13)), pltpu.SemaphoreType.DMA((count, 13)), pltpu.SemaphoreType.DMA((count,))],
        compiler_params=pltpu.CompilerParams(collective_id=collective_id, has_side_effects=True),
        cost_estimate=pl.CostEstimate(flops=0, bytes_accessed=2 * n * sum(s.size for s in shards), transcendentals=0),
    )(*shards)


def place_kernel(x_ref, *rest):
    rest[-1][0] = x_ref[...]


def place(x, which, into, rows):
    total, cols = x.shape
    extra = [] if into is None else [into]
    return pl.pallas_call(
        place_kernel,
        grid=(total // rows,),
        out_shape=jax.ShapeDtypeStruct((2, total, cols), x.dtype),
        in_specs=[pl.BlockSpec((rows, cols), lambda i: (i, 0))] + [ANY] * len(extra),
        out_specs=pl.BlockSpec((1, rows, cols), lambda i: (which, i, 0)),
        input_output_aliases={} if into is None else {1: 0},
        compiler_params=params(),
        cost_estimate=pl.CostEstimate(flops=x.size, bytes_accessed=4 * x.size, transcendentals=0),
    )(x, *extra)


def solution(mesh):
    n = mesh.shape["data"]
    batch_rows = P("data", None)
    state_rows = P(None, "data", None)
    replicated = P()

    def gather(x):
        return lax.all_gather(x, "data", axis=0, tiled=True)

    def device_body(act_in, grad_out, w_up, w_down, master_up, master_down, exp_avg_up, exp_avg_down, exp_sq_up, exp_sq_down, learn_rate, clip_norm):
        dim, ff = w_up.shape[1:]
        fs, ds = ff // n, dim // n
        me = lax.axis_index("data")
        e_all = gather(grad_out)
        x_all = gather(act_in)
        master_sq = jnp.concatenate([jnp.sum(master_up * master_up, axis=(1, 2)), jnp.sum(master_down * master_down, axis=(1, 2))])
        act_one = gelu_val(mm("td,df->tf", act_in, w_up[0])).astype(BF)
        hidden = mm("tf,fd->td", act_one, w_down[0]).astype(BF)
        h_all = gather(hidden)
        z_three = mm("td,df->tf", hidden, w_up[1])
        dz_three = (mm("td,fd->tf", grad_out, w_down[1]) * gelu_slope(z_three)).astype(BF)
        d_hidden = mm("tf,df->td", dz_three, w_up[1]).astype(BF)
        r_all = gather(d_hidden)
        up_slice = lax.dynamic_slice(w_up, (0, 0, me * fs), (2, dim, fs))
        down_slice = lax.dynamic_slice(w_down, (0, me * fs, 0), (2, fs, dim))

        def pair(x_in, up, down, cot):
            z = mm("df,td->ft", up, x_in)
            act = gelu_val(z).astype(BF)
            q = (mm("fd,td->ft", down, cot) * gelu_slope(z)).astype(BF)
            g_up = mm("td,ft->df", x_in, q) / n
            g_down = mm("ft,td->fd", act, cot) / n
            return g_up, g_down

        def exchange(g_up):
            return lax.all_to_all(g_up.reshape(n, ds, fs), "data", split_axis=0, concat_axis=0, tiled=False)

        g_three, g_four = pair(h_all, up_slice[1], down_slice[1], e_all)
        parts_three = exchange(g_three)
        g_one, g_two = pair(x_all, up_slice[0], down_slice[0], r_all)
        parts_one = exchange(g_one)
        local_sq = sum(jnp.sum(g * g) for g in (g_one, g_two, g_three, g_four))

        def tile(x):
            return jnp.where((lax.broadcasted_iota(jnp.int32, (8, 128), 0) + lax.broadcasted_iota(jnp.int32, (8, 128), 1)) == 0, x, 0.0)[None]

        grad_norm = jnp.sqrt(device_sums(tile(local_sq), n, 1)[0])
        scale = jnp.minimum(1.0, clip_norm / (grad_norm + NORM_EPS)).reshape(1)
        avg_down, sq_down, stat_down = moments_down(scale, g_two, g_four, exp_avg_down, exp_sq_down, 160)
        avg_up, sq_up, stat_three = moments_up(scale, parts_three, exp_avg_up, exp_sq_up, 1, None, 32)
        early = device_sums(jnp.concatenate([stat_down, stat_three, tile(master_sq[0]), tile(master_sq[1]), tile(master_sq[2]), tile(master_sq[3])]), n, 2)
        factor = lambda master_total, dir_total: (learn_rate * (jnp.sqrt(master_total) / jnp.sqrt(dir_total))).reshape(1)
        master_down_out, own_two = apply_update(factor(early[5], early[0]), master_down, avg_down, sq_down, 0, None, 160)
        new_two = gather(own_two)
        avg_up, sq_up, stat_one = moments_up(scale, parts_one, exp_avg_up, exp_sq_up, 0, (avg_up, sq_up), 32)
        late = device_sums(stat_one, n, 3)
        master_down_out, own_four = apply_update(factor(early[6], early[1]), master_down, avg_down, sq_down, 1, master_down_out, 160)
        master_up_out, own_three = apply_update(factor(early[4], early[2]), master_up, avg_up, sq_up, 1, None, 32)
        master_up_out, own_one = apply_update(factor(early[3], late[0]), master_up, avg_up, sq_up, 0, master_up_out, 32)
        new_four, new_three = gather_rows([own_four, own_three], n, 4)
        own_one, new_four, new_three = lax.optimization_barrier((own_one, new_four, new_three))
        new_one = gather(own_one)
        new_down = place(new_four, 1, place(new_two, 0, None, 640), 640)
        new_up = place(new_one, 0, place(new_three, 1, None, 128), 128)
        return (new_up, new_down, master_up_out, master_down_out, avg_up, avg_down, sq_up, sq_down, grad_norm)


    return jax.shard_map(device_body, mesh=mesh, in_specs=(batch_rows, batch_rows, replicated, replicated, state_rows, state_rows, state_rows, state_rows, state_rows, state_rows, replicated, replicated), out_specs=(replicated, replicated, state_rows, state_rows, state_rows, state_rows, state_rows, state_rows, replicated), check_vma=False)
```

time: 2180 us -> 1470 us (0.67)
  waiting for transfers between devices: 1270 us -> 413 us
  Pallas kernels: 0 us -> 471 us
  local copies, waits for them, and re-layouts: 279 us -> 23.4 us
  other arithmetic: 178 us -> 18.8 us
  matrix products: 380 us -> 508 us
  blocking collectives: 46.8 us -> 0 us
    reduce_scatter x2 -> x0, waiting for transfers between devices: 589 us -> none  [reduce_rows(): lax.psum_scatter(grad, 'data', scatter_dimension=0, tiled=True) / group_size]
    pallas_call x0 -> x15, Pallas kernels: none -> 471 us  [the longest x1 250 us: gather_rows(): pl.pallas_call(functools.partial(ag_kernel, count), out_shape=[jax.ShapeD...]
    unnamed x8 -> x6, waiting for transfers between devices: 304 us -> 1.44 us
    unnamed x35 -> x14, local copies, waits for them, and re-layouts: 261 us -> 4.73 us
    dot_general x9 -> x13, matrix products: 344 us -> 508 us  [mm(): return jnp.einsum(spec, lhs, rhs, preferred_element_type=jnp.float32)]
    all_to_all x0 -> x2, waiting for transfers between devices: none -> 109 us  [exchange(): lax.all_to_all(g_up.reshape(n, ds, fs), 'data', split_axis=0, concat_axis...]
    reduce_sum x6 -> x2, other arithmetic: 95.6 us -> 15.7 us  [the longest x1 8.49 us: device_body(): jnp.sum(master_up * master_up, axis=(1, 2))]
    all_gather x2 -> x6, waiting for transfers between devices: 377 us -> 302 us  [gather(): return lax.all_gather(x, 'data', axis=0, tiled=True)]
  transfers between devices with their start and end apart: 6 -> 8, of which waited for: 6 -> 5; matrix products, arithmetic and copies ran while one was open for 21% -> 32% of each run, Pallas kernels for 0% -> 28%
where the time goes in v1:
time: 1470 us
  matrix products  508 us (35%)
  Pallas kernels  471 us (32%)
  waiting for transfers between devices  413 us (28%)
  between operations  25.8 us (2%)
  local copies, waits for them, and re-layouts  23.4 us (2%)
  other arithmetic  18.8 us (1%)
    dot_general x13, matrix products, mm(): return jnp.einsum(spec, lhs, rhs, preferred_element_type=jnp.float32)  508 us
    all_gather x6, waiting for transfers between devices, gather(): return lax.all_gather(x, 'data', axis=0, tiled=True)  302 us
    pallas_call x1, Pallas kernels, gather_rows(): pl.pallas_call(functools.partial(ag_kernel, count), out_shape=[jax.ShapeD...  250 us
    all_to_all x2, waiting for transfers between devices, exchange(): lax.all_to_all(g_up.reshape(n, ds, fs), 'data', split_axis=0, concat_axis...  109 us
    pallas_call x4, Pallas kernels, place(): pl.pallas_call(place_kernel, grid=(total // rows,), out_shape=jax.ShapeDt...  90.2 us
    pallas_call x4, Pallas kernels, apply_update(): pl.pallas_call(apply_kernel, grid=(total // rows,), out_shape=(jax.ShapeD...  50.6 us
    pallas_call x2, Pallas kernels, moments_up(): pl.pallas_call(moments_up_kernel, grid=(total // rows,), out_shape=(jax.S...  31 us
  transfers between devices with their start and end apart: 8, of which 5 were waited for; matrix products, arithmetic and copies ran while one was open for 32% of the time, Pallas kernels for 28%

profile of v1, /device:TPU:0, one launch (start us, length us, event | category | flops | bytes accessed | tf_op | source)
XLA Modules:
  0.0 1467.9 jit_solution(2315458416941408672)
XLA Ops:
  7.2 33.8 %multiply_convert_fusion.15 = bf16[1024,8960]{1,0:T(8,128)(2,1)S(1)} fusion(bf16[1024,1536]{1,0:T(8,128)(2,1)} %param.12, bf16[2,1536,8960]{2,1,0:T(8,128)(2,1)} %param.14), kind=kOutput, calls=%fused_computation.25.clone.clone.clone.clone.2 | convolution fusion | flops 28231598080 | bytes 49020928 | tf_op jit(solution)/shard_map/td,df->tf/dot_general | solution.py:38
  41.1 32.7 %fusion.55 = bf16[1024,1536]{1,0:T(8,128)(2,1)} fusion(bf16[2,8960,1536]{2,1,0:T(8,128)(2,1)} %param.15, bf16[1024,8960]{1,0:T(8,128)(2,1)S(1)} %multiply_convert_fusion.15), kind=kOutput, calls=%fused_computation.60 | convolution fusion | flops 28187295744 | bytes 49020928 | tf_op jit(solution)/shard_map/tf,fd->td/dot_general | solution.py:38
  73.9 0.7 all-gather.13.cloned.1.call-update
  74.6 0.7 all-gather.9.cloned.1.call-update
  75.9 35.2 %fusion.28 = f32[1024,8960]{1,0:T(8,128)} fusion(bf16[1024,1536]{1,0:T(8,128)(2,1)S(1)} %copy-done.3, bf16[2,8960,1536]{2,1,0:T(8,128)(2,1)} %param.15), kind=kOutput, calls=%fused_computation.36 | convolution fusion | flops 28185722880 | bytes 67371008 | tf_op jit(solution)/shard_map/td,fd->tf/dot_general | solution.py:38
  111.1 43.8 %fusion.139 = bf16[1024,8960]{1,0:T(8,128)(2,1)} fusion(f32[1024,8960]{1,0:T(8,128)} %fusion.28, bf16[1024,1536]{1,0:T(8,128)(2,1)S(1)} %copy-done.4, bf16[2,1536,8960]{2,1,0:T(8,128)(2,1)} %param.14), kind=kOutput, calls=%fused_computation.8.clone.clone.clone.clone.2 | convolution fusion | flops 28277473280 | bytes 85721088 | tf_op jit(solution)/shard_map/td,df->tf/dot_general | solution.py:38
  154.8 35.4 %fusion.60 = bf16[1024,1536]{1,0:T(8,128)(2,1)} fusion(bf16[2,1536,8960]{2,1,0:T(8,128)(2,1)} %param.14, bf16[1024,8960]{1,0:T(8,128)(2,1)} %fusion.139), kind=kOutput, calls=%fused_computation.61 | convolution fusion | flops 28187295744 | bytes 49020928 | tf_op jit(solution)/shard_map/tf,df->td/dot_general | solution.py:38
  191.6 7.2 multiply_reduce_fusion
  199.3 8.5 multiply_reduce_fusion.1
  207.8 0.7 fusion.90
  208.5 43.2 %fusion.67 = f32[1120,8192]{1,0:T(8,128)} fusion(bf16[8192,1536]{1,0:T(8,128)(2,1)} %all-gather.11.cloned.1.call-done, bf16[2,1536,8960]{2,1,0:T(8,128)(2,1)} %param.14, s32[]{:T(128)S(6)} %add.90, s32[]{:T(128)S(6)} %select_n.55), kind=kOutput, calls=%fused_computation.63 | convolution fusion | flops 28185722880 | bytes 65404936 | tf_op jit(solution)/shard_map/df,td->ft/dot_general | solution.py:38
  251.6 66.3 %all-gather.13.cloned.1.call-done = bf16[8192,1536]{1,0:T(8,128)(2,1)} async-done(((bf16[1024,1536]{1,0:T(8,128)(2,1)}), bf16[8192,1536]{1,0:T(8,128)(2,1)}) %all-gather.13.cloned.1.call-update) | async-done | bytes 25165840 | tf_op jit(solution)/shard_map/all_gather | solution.py:296
  317.9 43.4 %fusion.17.clone.3.clone.4 = bf16[1120,8192]{1,0:T(8,128)(2,1)S(1)} fusion(f32[1120,8192]{1,0:T(8,128)} %fusion.67, bf16[8192,1536]{1,0:T(8,128)(2,1)} %all-gather.13.cloned.1.call-done, bf16[2,8960,1536]{2,1,0:T(8,128)(2,1)} %param.15, s32[]{:T(128)S(6)} %add.90, s32[]{:T(128)S(6)} %select_n.55), kind=kOutput, calls=%fused_computation.20.clone.clone.clone.clone.clone.clone.clone.1 | convolution fusion | flops 28277473280 | bytes 83656712 | tf_op jit(solution)/shard_map/fd,td->ft/dot_general | solution.py:38
  361.3 35.2 %multiply_reduce_fusion.3 = (f32[]{:T(128)}, f32[1536,1120]{0,1:T(8,128)}) fusion(bf16[8192,1536]{1,0:T(8,128)(2,1)} %all-gather.11.cloned.1.call-done, bf16[1120,8192]{1,0:T(8,128)(2,1)S(1)} %fusion.17.clone.3.clone.4), kind=kOutput, calls=%fused_computation.57 | convolution fusion | flops 28190883840 | bytes 50397188 | tf_op jit(solution)/shard_map/td,ft->df/dot_general | solution.py:38
  396.5 7.8 copy.27
  404.3 3.6 all-to-all-start
  407.9 75.8 %all-gather.9.cloned.1.call-done = bf16[8192,1536]{1,0:T(8,128)(2,1)} async-done(((bf16[1024,1536]{1,0:T(8,128)(2,1)}), bf16[8192,1536]{1,0:T(8,128)(2,1)}) %all-gather.9.cloned.1.call-update) | async-done | bytes 25165840 | tf_op jit(solution)/shard_map/all_gather | solution.py:296
  483.7 42.4 %fusion.68 = f32[1120,8192]{1,0:T(8,128)} fusion(bf16[8192,1536]{1,0:T(8,128)(2,1)} %all-gather.9.cloned.1.call-done, bf16[2,1536,8960]{2,1,0:T(8,128)(2,1)} %param.14, s32[]{:T(128)S(6)} %select_n.55), kind=kOutput, calls=%fused_computation.65 | convolution fusion | flops 28185722880 | bytes 65404932 | tf_op jit(solution)/shard_map/df,td->ft/dot_general | solution.py:38
  526.1 98.6 %all-gather.7.cloned.1.call-done = bf16[8192,1536]{1,0:T(8,128)(2,1)} async-done(((bf16[1024,1536]{1,0:T(8,128)(2,1)}), bf16[8192,1536]{1,0:T(8,128)(2,1)}) %all-gather.7.cloned.1.call-update) | async-done | bytes 25165840 | tf_op jit(solution)/shard_map/all_gather | solution.py:296
  624.7 42.0 %multiply_reduce_fusion.4 = (f32[]{:T(128)}, f32[1120,1536]{1,0:T(8,128)}) fusion(bf16[8192,1536]{1,0:T(8,128)(2,1)} %all-gather.7.cloned.1.call-done, f32[1120,8192]{1,0:T(8,128)} %fusion.68), kind=kOutput, calls=%fused_computation.58 | convolution fusion | flops 28236759040 | bytes 68747264 | tf_op jit(solution)/shard_map/ft,td->fd/dot_general | solution.py:38
  666.7 43.3 %fusion.11.clone.5.clone.4 = bf16[1120,8192]{1,0:T(8,128)(2,1)S(1)} fusion(f32[1120,8192]{1,0:T(8,128)} %fusion.68, bf16[8192,1536]{1,0:T(8,128)(2,1)} %all-gather.7.cloned.1.call-done, bf16[2,8960,1536]{2,1,0:T(8,128)(2,1)} %param.15, s32[]{:T(128)S(6)} %select_n.55), kind=kOutput, calls=%fused_computation.14.clone.clone.clone.clone.clone.clone.clone.clone.clone.1 | convolution fusion | flops 28277473280 | bytes 83656704 | tf_op jit(solution)/shard_map/fd,td->ft/dot_general | solution.py:38
  710.0 35.4 %multiply_reduce_fusion.5 = (f32[]{:T(128)}, f32[1536,1120]{0,1:T(8,128)}) fusion(bf16[8192,1536]{1,0:T(8,128)(2,1)} %all-gather.9.cloned.1.call-done, bf16[1120,8192]{1,0:T(8,128)(2,1)S(1)} %fusion.11.clone.5.clone.4), kind=kOutput, calls=%fused_computation.59 | convolution fusion | flops 28190883840 | bytes 50397188 | tf_op jit(solution)/shard_map/td,ft->df/dot_general | solution.py:38
  747.4 42.1 %multiply_reduce_fusion.2 = (f32[]{:T(128)}, f32[1120,1536]{1,0:T(8,128)}) fusion(bf16[8192,1536]{1,0:T(8,128)(2,1)} %all-gather.13.cloned.1.call-done, f32[1120,8192]{1,0:T(8,128)} %fusion.67), kind=kOutput, calls=%fused_computation.56 | convolution fusion | flops 28236759040 | bytes 68747264 | tf_op jit(solution)/shard_map/ft,td->fd/dot_general | solution.py:38
  790.7 6.1 shard_map.187
  797.6 29.3 %moments_down.1 = (f32[2,1120,1536]{2,1,0:T(8,128)}, f32[2,1120,1536]{2,1,0:T(8,128)}, f32[2,8,128]{2,1,0:T(8,128)S(1)}) custom-call(f32[1]{0:T(128)} %bitcast.10.s_ref, f32[1120,1536]{1,0:T(8,128)} %get-tuple-element.67.ga_ref, f32[1120,1536]{1,0:T(8,128)} %get-tuple-element.71.gb_ref, f32[2,1120,1536]{2,1,0:T(8,128)} %m_ref.3, f32[2,1120,1536]{2,1,0:T(8,128)} %v_ref.3), custom_call_target="tpu_custom_call" | custom-call | flops 137625600 | bytes 68812800 | tf_op jit(solution)/shard_map/moments_down/pallas_call | solution.py:114
  826.9 14.8 %shard_map.188 = (f32[2,192,8960]{2,1,0:T(8,128)}, f32[2,192,8960]{2,1,0:T(8,128)}, f32[1,8,128]{2,1,0:T(8,128)S(1)}) custom-call(f32[1]{0:T(128)} %bitcast.10.s_ref, f32[8,192,1120]{2,1,0:T(8,128)} %all-to-all-done.g_ref, f32[2,192,8960]{2,1,0:T(8,128)} %m_ref.5, f32[2,192,8960]{2,1,0:T(8,128)} %v_ref.5), custom_call_target="tpu_custom_call" | custom-call | flops 68812800 | bytes 34406400 | tf_op jit(solution)/shard_map/pallas_call | solution.py:142
  841.7 0.6 constant_dynamic-update-slice_fusion.3
  842.4 0.7 constant_dynamic-update-slice_fusion.2
  843.1 0.6 constant_dynamic-update-slice_fusion.1
  844.9 7.6 shard_map.189
  852.5 1.6 fusion.88
  855.5 13.8 shard_map.194
  869.3 8.0 copy.28
  877.3 3.6 all-to-all-start.1
  884.2 109.5 %all-to-all-done.1.g_ref = f32[8,192,1120]{2,1,0:T(8,128)} async-done(((f32[8,192,1120]{2,1,0:T(8,128)}), f32[8,192,1120]{2,1,0:T(8,128)}, u32[]{:S(2)}, u32[]{:S(2)}) %all-to-all-start.1) | async-done | bytes 6881312 | tf_op jit(solution)/shard_map/all_to_all | solution.py:324
  993.7 16.2 %shard_map.190 = (f32[2,192,8960]{2,1,0:T(8,128)}, f32[2,192,8960]{2,1,0:T(8,128)}, f32[1,8,128]{2,1,0:T(8,128)S(1)}) custom-call(f32[1]{0:T(128)} %bitcast.10.s_ref, f32[8,192,1120]{2,1,0:T(8,128)} %all-to-all-done.1.g_ref, f32[2,192,8960]{2,1,0:T(8,128)} %m_ref.5, f32[2,192,8960]{2,1,0:T(8,128)} %v_ref.5, ...), custom_call_target="tpu_custom_call", output_to_operand_aliasing={{0}: (4, {}), {1}: (5, {})} | custom-call | flops 68812800 | bytes 34406400 | tf_op jit(solution)/shard_map/pallas_call | solution.py:142
  1010.4 6.3 shard_map.191
  1017.5 12.5 shard_map.195
  1030.0 1.8 copy-done
  1031.8 11.7 shard_map.192
  1043.5 1.8 copy-done.1
  1045.2 250.3 %shard_map.196 = (bf16[8960,1536]{1,0:T(8,128)(2,1)}, bf16[1536,8960]{1,0:T(8,128)(2,1)}) custom-call(bf16[1120,1536]{1,0:T(8,128)(2,1)} %copy-done, bf16[192,8960]{1,0:T(8,128)(2,1)} %copy-done.1), custom_call_target="tpu_custom_call" | custom-call | bytes 55050240 | tf_op jit(solution)/shard_map/pallas_call | solution.py:259
  1295.5 12.5 shard_map.193
  1308.1 22.4 %shard_map.197.rest_0_ = bf16[2,1536,8960]{2,1,0:T(8,128)(2,1)} custom-call(bf16[1536,8960]{1,0:T(8,128)(2,1)} %get-tuple-element.48.x_ref), custom_call_target="tpu_custom_call" | custom-call | flops 13762560 | bytes 55050240 | tf_op jit(solution)/shard_map/pallas_call | solution.py:277
  1330.4 22.8 %shard_map.199.rest_0_ = bf16[2,8960,1536]{2,1,0:T(8,128)(2,1)} custom-call(bf16[8960,1536]{1,0:T(8,128)(2,1)} %all-gather.17.cloned.1.call-done.x_ref), custom_call_target="tpu_custom_call" | custom-call | flops 13762560 | bytes 55050240 | tf_op jit(solution)/shard_map/pallas_call | solution.py:277
  1353.2 23.3 %shard_map.200 = bf16[2,8960,1536]{2,1,0:T(8,128)(2,1)} custom-call(bf16[8960,1536]{1,0:T(8,128)(2,1)} %get-tuple-element.49.x_ref, bf16[2,8960,1536]{2,1,0:T(8,128)(2,1)} %shard_map.199.rest_0_), custom_call_target="tpu_custom_call", output_to_operand_aliasing={{}: (1, {})} | custom-call | flops 13762560 | bytes 55050240 | tf_op jit(solution)/shard_map/pallas_call | solution.py:277
  1376.5 61.1 %all-gather.15.cloned.1.call-done.x_ref = bf16[1536,8960]{1,0:T(8,128)(2,1)} async-done(((bf16[192,8960]{1,0:T(8,128)(2,1)}), bf16[1536,8960]{1,0:T(8,128)(2,1)}) %all-gather.15.cloned.1.call-update) | async-done | bytes 27525136 | tf_op jit(solution)/shard_map/all_gather | solution.py:296
  1437.6 21.8 %shard_map.198 = bf16[2,1536,8960]{2,1,0:T(8,128)(2,1)} custom-call(bf16[1536,8960]{1,0:T(8,128)(2,1)} %all-gather.15.cloned.1.call-done.x_ref, bf16[2,1536,8960]{2,1,0:T(8,128)(2,1)} %shard_map.197.rest_0_), custom_call_target="tpu_custom_call", output_to_operand_aliasing={{}: (1, {})} | custom-call | flops 13762560 | bytes 55050240 | tf_op jit(solution)/shard_map/pallas_call | solution.py:277
  (28 shorter events, 3.8 us)
Async XLA Ops:
  7.2 201.3 %all-gather.11.cloned.1.call-start = ((), (), s32[]{:S(2)}) async-start(), calls=%async_computation.4 | async-start | bytes 28311552 | tf_op jit(solution)/shard_map/all_gather | solution.py:296
  41.1 34.8 %copy-start.3 = (bf16[1024,1536]{1,0:T(8,128)(2,1)S(1)}, bf16[1024,1536]{1,0:T(8,128)(2,1)}, u32[]{:S(2)}) copy-start(bf16[1024,1536]{1,0:T(8,128)(2,1)} %param.13) | copy-start | bytes 9437188
  73.8 244.1 %all-gather.13.cloned.1.call-start = ((), (), s32[]{:S(2)}) async-start(), calls=%async_computation.5 | async-start | bytes 28311552 | tf_op jit(solution)/shard_map/all_gather | solution.py:296
  74.6 409.1 %all-gather.9.cloned.1.call-start = ((), (), s32[]{:S(2)}) async-start(), calls=%async_computation.3 | async-start | bytes 28311552 | tf_op jit(solution)/shard_map/all_gather | solution.py:296
  75.3 549.4 %all-gather.7.cloned.1.call-start = ((), (), s32[]{:S(2)}) async-start(), calls=%async_computation.2 | async-start | bytes 28311552 | tf_op jit(solution)/shard_map/all_gather | solution.py:296
  75.9 35.2 %copy-start.4 = (bf16[1024,1536]{1,0:T(8,128)(2,1)S(1)}, bf16[1024,1536]{1,0:T(8,128)(2,1)}, u32[]{:S(2)}) copy-start(bf16[1024,1536]{1,0:T(8,128)(2,1)} %fusion.55) | copy-start | bytes 9437188
  404.3 422.6 %all-to-all-start = ((f32[8,192,1120]{2,1,0:T(8,128)}), f32[8,192,1120]{2,1,0:T(8,128)}, u32[]{:S(2)}, u32[]{:S(2)}) async-start(f32[8,192,1120]{2,1,0:T(8,128)} %bitcast.118), calls=%async_computation | async-start | bytes 14155776 | tf_op jit(solution)/shard_map/all_to_all | solution.py:324
  407.9 922.6 %all-gather.17.cloned.1.call-start = ((), (), s32[]{:S(2)}) async-start(), calls=%async_computation.7 | async-start | bytes 30965760 | tf_op jit(solution)/shard_map/all_gather | solution.py:296
  844.3 0.6 copy-start.5
  877.3 116.3 %all-to-all-start.1 = ((f32[8,192,1120]{2,1,0:T(8,128)}), f32[8,192,1120]{2,1,0:T(8,128)}, u32[]{:S(2)}, u32[]{:S(2)}) async-start(f32[8,192,1120]{2,1,0:T(8,128)} %bitcast.119), calls=%async_computation.1 | async-start | bytes 14155776 | tf_op jit(solution)/shard_map/all_to_all | solution.py:324
  881.0 556.7 %all-gather.15.cloned.1.call-start = ((), (), s32[]{:S(2)}) async-start(), calls=%async_computation.6 | async-start | bytes 30965760 | tf_op jit(solution)/shard_map/all_gather | solution.py:296
  1009.8 0.6 copy-start.2
  1030.0 1.8 copy-start
  1043.5 1.8 copy-start.1
Sparse Core Ops, SparseCore 0:
  74.0 122.4 all-gather.10
  198.2 119.6 all-gather.12
  319.7 163.9 all-gather.8
  486.0 138.7 all-gather.6
  869.4 220.7 all-gather.16
  1308.2 129.4 all-gather.14
